TPU v7x, 32 devices: a whole 2x2x4 slice. The times are simulated.
32 devices in a mesh: tm: 4 (over y, x), sat: 8 (over z, core).
Axes of the slice: x: 2, y: 2, z: 4, core: 2. Of those that a mesh axis runs over, the one named last changes fastest.
Arguments:
- samples: int32 [2, 8, 8192], P(None, 'tm', 'sat'), may hold values from -1073741824 to 1073741823
- codes: int32 [24, 4092], P('sat'), may hold values from -1 to 1, as said below
- dopplers: int32 [16], replicated, may hold values from -60 to 60
Outputs:
- power: float32 [16, 24, 8192], P('tm', 'sat')
- detection: float32 [24], P('sat')
Inputs may be any that keep to these rules, and one draw needn't show every extreme that they name: `codes`: each entry is -1 or 1.
All inputs are finite; a program needn't handle non-finite values.
Results may differ from a plain program's by a relative error of at most 0.0003.
Values sent between devices are 32-bit elements.
A program may use at most 64 MiB of HBM per device.

v0:
```python
import functools
import math

import jax
import jax.numpy as jnp
import ml_dtypes
import numpy as np
from jax import lax
from jax.experimental import pallas as pl
from jax.experimental.pallas import tpu as pltpu
from jax.sharding import PartitionSpec as P

sample_scale = 2.0 ** (-29)
wrap_count = 32768
LANES = 128
KERNEL_BYTES = 55_800_000
PADDING = 1_200_000
MESH = pl.DeviceIdType.MESH


def halves(table):
    high = table.astype(np.float32).astype(ml_dtypes.bfloat16)
    low = (table - high.astype(np.float64)).astype(np.float32).astype(ml_dtypes.bfloat16)
    return high, low


@functools.lru_cache(maxsize=None)
def tables(sample_length, chip_count):
    inner = LANES
    outer = sample_length // inner
    a = np.arange(outer)
    c = np.arange(inner)
    ang_o = 2 * np.pi * (np.outer(a, a) % outer) / outer
    ang_t = 2 * np.pi * (np.outer(a, c) % sample_length) / sample_length
    ang_i = 2 * np.pi * (np.outer(c, c) % inner) / inner
    fc, fs = np.cos(ang_o), -np.sin(ang_o)
    first = np.block([[fc, -fs], [fs, fc]])
    second = np.block([[-fs, -fc], [fc, -fs]])
    wc, ws = np.cos(ang_i), -np.sin(ang_i)
    fh, fl = halves(np.block([[wc, ws], [-ws, wc]]))
    ih, il = halves(np.block([[wc, -ws], [ws, wc]]))
    bh, bl = halves(np.block([[fc, fs], [-fs, fc]]))
    ch, cl = halves(np.concatenate([fc, fs], axis=0))
    offsets = np.arange(sample_length).reshape(outer, inner)
    chips = offsets * chip_count // sample_length
    signs = 1 - 2 * ((offsets * 2 * chip_count // sample_length) % 2)
    starts = tuple(int(v) for v in chips[:, 0])
    within = chips - chips[:, :1]
    wide = np.concatenate([fh, fh, fl, ih, ih, il], axis=0)
    narrow = [first, second, np.cos(ang_t), -np.sin(ang_t), bh, bl,
              np.concatenate([ch, cl], axis=1), within, signs]
    narrow = np.concatenate([np.asarray(t, np.float32) for t in narrow], axis=0)
    return wide, narrow, starts


def padded(table, size):
    extra = -(-size // (table.shape[1] * table.dtype.itemsize)) - table.shape[0]
    return np.pad(table, ((0, max(extra, 0)), (0, 0)))


def split(value):
    high = value.astype(jnp.bfloat16)
    low = (value - high.astype(jnp.float32)).astype(jnp.bfloat16)
    return high, low


def mm(left, right):
    return jnp.dot(left, right, preferred_element_type=jnp.float32)


def kernel(starts, outer, chip_count, cores, x_ref, codes_ref, dop_ref, wide_hbm, narrow_hbm,
           power_ref, peak_ref, raw, chips, wide, narrow, back,
           everyone, cpad, gath, cspec, rot, dtw, energy, acc, peaks, mine,
           tab_sem, send1, recv1, send2, recv2, send3, recv3, send4, recv4):
    inner = LANES
    tm_count, _, line, _, own, rows, _ = everyone.shape
    sat_count = cores * line
    blocks = tm_count * own
    dop_rows, sats = acc.shape[0], acc.shape[1]
    sample_length = outer * inner
    me_tm, me_sat = lax.axis_index("tm"), lax.axis_index("sat")
    me_z, me_core = me_sat // cores, lax.rem(me_sat, cores)
    twin = me_z * cores + (cores - 1 - me_core)

    paired = tm_count & (tm_count - 1) == 0

    def tm_peer(k):
        if not paired:
            return lax.rem(me_tm + k, tm_count)
        peer, bit = 0, 1
        while bit < tm_count:
            peer = peer + ((me_tm // bit + k // bit) % 2) * bit
            bit *= 2
        return peer

    def tm_source(k):
        return tm_peer(k) if paired else lax.rem(me_tm + tm_count - k, tm_count)

    def z_peer(k):
        return lax.rem(me_z + k, line)

    def z_source(k):
        return lax.rem(me_z + line - k, line)

    barrier = pltpu.get_barrier_semaphore()
    for k in range(1, line):
        pl.semaphore_signal(barrier, inc=1, device_id={"sat": z_peer(k) * cores + me_core}, device_id_type=MESH)
    for k in range(1, tm_count):
        pl.semaphore_signal(barrier, inc=1, device_id={"tm": tm_peer(k)}, device_id_type=MESH)
    if cores > 1:
        pl.semaphore_signal(barrier, inc=1, device_id={"sat": twin}, device_id_type=MESH)

    pairs = ((x_ref, raw), (codes_ref, chips),
             (narrow_hbm.at[pl.ds(0, narrow.shape[0])], narrow),
             (wide_hbm.at[pl.ds(0, wide.shape[0])], wide))
    loads = [pltpu.make_async_copy(h, t, tab_sem.at[i]) for i, (h, t) in enumerate(pairs)]
    for load in loads:
        load.start()
    loads[0].wait()
    for part in range(2):
        for r in range(rows):
            piece = raw[part, :, r * LANES:(r + 1) * LANES]
            for blk in range(own):
                everyone[me_tm, me_core, me_z, part, blk, r:r + 1, :] = piece[blk:blk + 1]
    loads[1].wait()

    cpad[...] = jnp.zeros_like(cpad)
    cpad[0:sats, 0:chip_count] = chips[...].astype(jnp.float32)
    for n1 in range(outer):
        base = starts[n1] // LANES * LANES
        shift = starts[n1] - base
        piece = cpad[:, base:base + 2 * LANES]
        if shift:
            piece = pltpu.roll(piece, 2 * LANES - shift, 1)
        for s in range(sats):
            gath[s, n1:n1 + 1, :] = piece[s:s + 1, :LANES]

    pl.semaphore_wait(barrier, line + tm_count + cores - 3)

    def along_z(k, at):
        return pltpu.make_async_remote_copy(
            src_ref=everyone.at[me_tm, me_core, me_z], dst_ref=everyone.at[me_tm, me_core, at],
            send_sem=send1.at[k - 1], recv_sem=recv1.at[k - 1],
            device_id={"sat": z_peer(k) * cores + me_core}, device_id_type=MESH)

    def along_tm(k, at):
        return pltpu.make_async_remote_copy(
            src_ref=everyone.at[me_tm, me_core], dst_ref=everyone.at[at, me_core],
            send_sem=send2.at[k - 1], recv_sem=recv2.at[k - 1],
            device_id={"tm": tm_peer(k)}, device_id_type=MESH)

    def to_twin(k, at_core):
        g = tm_source(k)
        return pltpu.make_async_remote_copy(
            src_ref=everyone.at[g, me_core], dst_ref=everyone.at[g, at_core],
            send_sem=send4.at[k], recv_sem=recv4.at[k],
            device_id={"sat": twin}, device_id_type=MESH)

    def share_peak(k):
        return pltpu.make_async_remote_copy(
            src_ref=mine, dst_ref=peaks.at[k - 1], send_sem=send3.at[k - 1],
            recv_sem=recv3.at[k - 1], device_id={"tm": tm_peer(k)}, device_id_type=MESH)

    for k in range(1, line):
        along_z(k, me_z).start()
    loads[2].wait()
    loads[3].wait()

    cut = [0]

    def take(count):
        cut.append(cut[-1] + count)
        return narrow[cut[-2]:cut[-1]]

    first, second = take(2 * outer), take(2 * outer)
    t_re, t_im = take(outer), take(outer)
    bh, bl = take(2 * outer).astype(jnp.bfloat16), take(2 * outer).astype(jnp.bfloat16)
    back[...] = jnp.concatenate([bh, bh, bl], axis=1)
    code = take(2 * outer).astype(jnp.bfloat16)
    within = take(outer).astype(jnp.int32)
    signs = take(outer)
    t_at = 4 * outer
    fwd_ref = wide.at[pl.ds(0, 6 * inner)]
    inv_ref = wide.at[pl.ds(6 * inner, 6 * inner)]
    scale = math.sqrt(1.0 / (float(sample_length) ** 3 * blocks))
    for s in range(sats):
        rep = jnp.take_along_axis(gath[s], within, axis=1) * signs
        rep = rep.astype(jnp.bfloat16)
        y = mm(code, jnp.concatenate([rep, rep], axis=0))
        y_re, y_im = y[:outer], y[outer:]
        z = jnp.concatenate([y_re * t_re - y_im * t_im, y_re * t_im + y_im * t_re], axis=1)
        zh, zl = split(z)
        cspec[s] = mm(jnp.concatenate([zh, zl, zh], axis=1), fwd_ref[...]) * scale

    lane = lax.broadcasted_iota(jnp.int32, (8, inner), 1)
    row_of = lax.rem(lane, outer) * inner
    base_row = me_tm * dop_rows
    turn = 2.0 * math.pi / wrap_count
    bins = lax.broadcasted_iota(jnp.int32, (8, inner), 0)
    for f0 in range(0, dop_rows, 4):
        d = jnp.zeros((8, inner), jnp.int32)
        for f in range(f0, min(f0 + 4, dop_rows)):
            d = jnp.where(lax.rem(bins, 4) == f - f0, dop_ref[base_row + f], d)
        m = (jnp.where(bins < 4, row_of, lane) * d) & (wrap_count - 1)
        angle = m.astype(jnp.float32) * turn
        cosine, sine = jnp.cos(angle), -jnp.sin(angle)
        for f in range(f0, min(f0 + 4, dop_rows)):
            i = f - f0
            c1, s1 = cosine[i:i + 1], sine[i:i + 1]
            c2, s2 = cosine[i + 4:i + 5], sine[i + 4:i + 5]
            mh, ml = split(first * c1 + second * s1)
            rot[f] = jnp.concatenate([mh, mh, ml], axis=1)
            dtw[f, 0] = t_re * c2 - t_im * s2
            dtw[f, 1] = t_re * s2 + t_im * c2

    energy[...] = jnp.zeros_like(energy)
    acc[...] = jnp.zeros_like(acc)
    for k in range(1, line):
        along_z(k, z_source(k)).wait_recv()
    for k in range(1, tm_count):
        along_tm(k, me_tm).start()
    if cores > 1:
        to_twin(0, me_core).start()

    def group(j, carry):
        @pl.when(j == 1)
        def _():
            along_tm(j, tm_source(j)).wait_recv()
            if cores > 1:
                to_twin(j, me_core).start()

        @pl.when((j > 0) & (j < tm_count - 1))
        def _():
            along_tm(j + 1, tm_source(j + 1)).wait_recv()
            if cores > 1:
                to_twin(j + 1, me_core).start()

        if cores > 1:
            to_twin(j, cores - 1 - me_core).wait_recv()
        g = tm_source(j)
        w_re, w_im = narrow[t_at:t_at + outer], narrow[t_at + outer:t_at + 2 * outer]
        cols = []
        for blk in range(own):
            parts = [everyone[g, q % cores, q // cores, part, blk] for part in range(2) for q in range(sat_count)]
            cols.append(jnp.concatenate(parts, axis=0))
        x = jnp.concatenate(cols, axis=1).astype(jnp.float32) * sample_scale
        sq = x * x
        energy[...] += jnp.sum(sq.reshape(2 * outer // 8, 8, own * inner), axis=0)
        xh, xl = split(x)
        xs = jnp.concatenate([xh, xl, xh], axis=0)
        for f in range(dop_rows):
            y = mm(rot[f], xs)
            u_re, u_im = dtw[f, 0], dtw[f, 1]
            zs = []
            for blk in range(own):
                y_re = y[:outer, blk * inner:(blk + 1) * inner]
                y_im = y[outer:, blk * inner:(blk + 1) * inner]
                zs.append(jnp.concatenate([y_re * u_re - y_im * u_im, y_re * u_im + y_im * u_re], axis=1))
            zh, zl = split(jnp.concatenate(zs, axis=0))
            spec = mm(jnp.concatenate([zh, zl, zh], axis=1), fwd_ref[...])
            crosses = []
            for s in range(sats):
                k_re, k_im = cspec[s, :, :inner], cspec[s, :, inner:]
                for blk in range(own):
                    s_re = spec[blk * outer:(blk + 1) * outer, :inner]
                    s_im = spec[blk * outer:(blk + 1) * outer, inner:]
                    crosses.append(jnp.concatenate(
                        [s_re * k_re + s_im * k_im, s_im * k_re - s_re * k_im], axis=1))
            ch, cl = split(jnp.concatenate(crosses, axis=0))
            lag = mm(jnp.concatenate([ch, cl, ch], axis=1), inv_ref[...])
            for s in range(sats):
                cols = []
                for blk in range(own):
                    at = (s * own + blk) * outer
                    l_re, l_im = lag[at:at + outer, :inner], lag[at:at + outer, inner:]
                    cols.append(jnp.concatenate(
                        [l_re * w_re + l_im * w_im, l_im * w_re - l_re * w_im], axis=0))
                wh, wl = split(jnp.concatenate(cols, axis=1))
                out = mm(back[...], jnp.concatenate([wh, wl, wh], axis=0))
                o_re, o_im = out[:outer], out[outer:]
                p = o_re * o_re + o_im * o_im
                total = p[:, :inner]
                for blk in range(1, own):
                    total = total + p[:, blk * inner:(blk + 1) * inner]
                acc[f, s] += total
        return carry

    lax.fori_loop(0, tm_count, group, 0)

    mine[...] = jnp.zeros_like(mine)
    for s in range(sats):
        top = acc[0, s]
        for f in range(1, dop_rows):
            top = jnp.maximum(top, acc[f, s])
        mine[s:s + 1, :] = jnp.max(top, axis=0, keepdims=True)
    for k in range(1, line):
        along_z(k, me_z).wait_send()
    for k in range(1, tm_count):
        along_tm(k, me_tm).wait_send()
    if cores > 1:
        for k in range(tm_count):
            to_twin(k, me_core).wait_send()
    for f in range(dop_rows):
        for s in range(sats):
            power_ref[s, :, f, :] = acc[f, s]
    for k in range(1, tm_count):
        share_peak(k).start()
    mean = jnp.sum(energy[...]) * (1.0 / float(blocks * sample_length))
    floor = jnp.maximum(mean, 0.25)
    for k in range(1, tm_count):
        share_peak(k).wait()
    best = mine[...]
    for k in range(1, tm_count):
        best = jnp.maximum(best, peaks[k - 1])
    best = jnp.max(best, axis=1, keepdims=True)
    peak_ref[...] = jnp.broadcast_to(best / floor, peak_ref.shape)


def shards(samples, codes, dopplers):
    tm_count, sat_count = lax.axis_size("tm"), lax.axis_size("sat")
    own, segment = samples.shape[1], samples.shape[2]
    sample_length = segment * sat_count
    outer, rows = sample_length // LANES, segment // LANES
    sats, chip_count = codes.shape
    dop_rows = dopplers.shape[0] // tm_count
    cores = 2 if sat_count % 2 == 0 else 1
    line = sat_count // cores
    wide, narrow, starts = tables(sample_length, chip_count)
    pad = (max(starts) // LANES + 2) * LANES
    pad = max(pad, -(-chip_count // LANES) * LANES)
    peak_rows = -(-sats // 8) * 8
    vm = pl.BlockSpec(memory_space=pltpu.VMEM)
    hbm = pl.BlockSpec(memory_space=pltpu.HBM)
    dma = pltpu.SemaphoreType.DMA
    power, peak = pl.pallas_call(
        functools.partial(kernel, starts, outer, chip_count, cores),
        out_shape=(
            jax.ShapeDtypeStruct((sats, outer, dop_rows, LANES), jnp.float32),
            jax.ShapeDtypeStruct((peak_rows, LANES), jnp.float32),
        ),
        in_specs=[hbm, hbm, pl.BlockSpec(memory_space=pltpu.SMEM), hbm, hbm],
        out_specs=(vm, vm),
        scratch_shapes=[
            pltpu.VMEM(samples.shape, jnp.int32),
            pltpu.VMEM(codes.shape, jnp.int32),
            pltpu.VMEM(wide.shape, jnp.bfloat16),
            pltpu.VMEM(narrow.shape, jnp.float32),
            pltpu.VMEM((2 * outer, 6 * outer), jnp.bfloat16),
            pltpu.VMEM((tm_count, cores, line, 2, own, rows, LANES), jnp.int32),
            pltpu.VMEM((8, pad), jnp.float32),
            pltpu.VMEM((sats, outer, LANES), jnp.float32),
            pltpu.VMEM((sats, outer, 2 * LANES), jnp.float32),
            pltpu.VMEM((dop_rows, 2 * outer, 6 * outer), jnp.bfloat16),
            pltpu.VMEM((dop_rows, 2, outer, LANES), jnp.float32),
            pltpu.VMEM((8, own * LANES), jnp.float32),
            pltpu.VMEM((dop_rows, sats, outer, LANES), jnp.float32),
            pltpu.VMEM((tm_count - 1, peak_rows, LANES), jnp.float32),
            pltpu.VMEM((peak_rows, LANES), jnp.float32),
            dma((4,)),
            dma((line - 1,)),
            dma((line - 1,)),
            dma((tm_count - 1,)),
            dma((tm_count - 1,)),
            dma((tm_count - 1,)),
            dma((tm_count - 1,)),
            dma((tm_count,)),
            dma((tm_count,)),
        ],
        compiler_params=pltpu.CompilerParams(
            vmem_limit_bytes=KERNEL_BYTES, collective_id=0, has_side_effects=True),
        name="search",
    )(samples, codes, dopplers, jnp.asarray(padded(wide, PADDING)), jnp.asarray(padded(narrow, PADDING)))
    power = power.transpose(2, 0, 1, 3).reshape(dop_rows, sats, sample_length)
    return power, peak[:sats, 0]


def solution(mesh):
    placed = (P(None, "tm", "sat"), P("sat", None), P())
    return jax.shard_map(
        shards,
        mesh=mesh,
        in_specs=placed,
        out_specs=(P("tm", "sat", None), P("sat")),
        check_vma=False,
    )
```

profile of v0, /device:TPU:0, one launch (start us, length us, event | category | flops | bytes accessed | tf_op | source)
XLA Modules:
  0.0 35.2 jit_solution(1591641031031337676)
XLA Ops:
  0.6 0.0 copy-start
  0.6 0.8 %copy-done = s32[3,4092]{1,0:T(4,128)S(1)} copy-done((s32[3,4092]{1,0:T(4,128)S(1)}, s32[3,4092]{1,0:T(4,128)}, u32[]{:S(2)}) %copy-start) | copy-done | bytes 49128
  1.5 0.0 copy-start.1
  1.5 0.7 %copy-done.1 = s32[2,2,1024]{2,1,0:T(2,128)S(1)} copy-done((s32[2,2,1024]{2,1,0:T(2,128)S(1)}, s32[2,2,1024]{2,1,0:T(2,128)}, u32[]{:S(2)}) %copy-start.1) | copy-done | bytes 16408
  2.2 0.0 copy-start.2
  2.2 0.7 %copy-done.2 = s32[16]{0:T(128)S(1)} copy-done((s32[16]{0:T(128)S(1)}, s32[16]{0:T(128)}, u32[]{:S(2)}) %copy-start.2) | copy-done | bytes 88
  2.8 31.0 %search.1 = (f32[3,64,4,128]{3,2,1,0:T(4,128)S(1)}, f32[8,128]{1,0:T(8,128)S(1)}) custom-call(s32[2,2,1024]{2,1,0:T(2,128)S(1)} %copy-done.1, s32[3,4092]{1,0:T(4,128)S(1)} %copy-done, s32[16]{0:T(128)S(1)} %copy-done.2, bf16[2344,256]{1,0:T(8,128)(2,1)} %constant.4.clone.wide_hbm, f32[2344,128]{1,0:T(8,128)} %constant.5.clone.narrow_hbm), custom_call_target="tpu_custom_call" | custom-call | tf_op jit(solution)/shard_map/search/pallas_call | solution.py:335
  33.9 0.6 %slice_reduce_fusion = f32[3]{0:T(128)} fusion(f32[8,128]{1,0:T(8,128)S(1)} %get-tuple-element.5), kind=kLoop, calls=%fused_computation | loop fusion | bytes 24 | tf_op jit(solution)/shard_map/slice | solution.py:374
  34.5 0.7 %copy.8 = f32[4,3,8192]{2,0,1:T(4,128)} copy(f32[4,3,8192]{2,0,1:T(4,128)S(1)} %bitcast.3) | data formatting | bytes 786432
Async XLA Ops:
  0.6 0.8 %copy-start = (s32[3,4092]{1,0:T(4,128)S(1)}, s32[3,4092]{1,0:T(4,128)}, u32[]{:S(2)}) copy-start(s32[3,4092]{1,0:T(4,128)} %codes_ref.1) | copy-start | bytes 147316
  1.5 0.7 %copy-start.1 = (s32[2,2,1024]{2,1,0:T(2,128)S(1)}, s32[2,2,1024]{2,1,0:T(2,128)}, u32[]{:S(2)}) copy-start(s32[2,2,1024]{2,1,0:T(2,128)} %x_ref.1) | copy-start | bytes 49156
  2.2 0.7 %copy-start.2 = (s32[16]{0:T(128)S(1)}, s32[16]{0:T(128)}, u32[]{:S(2)}) copy-start(s32[16]{0:T(128)} %dop_ref.1) | copy-start | bytes 196
where the time goes:
time: 35.5 us; the launch traced here: 35.2 us
  Pallas kernels  31 us (87%)
  local copies, waits for them, and re-layouts  3.58 us (10%)
  between operations  0.65 us (2%)
    pallas_call x1, Pallas kernels, shards(): pl.pallas_call(functools.partial(kernel, starts, outer, chip_count, cores...  31 us
    unnamed x7, local copies, waits for them, and re-layouts  2.95 us

commit v1 on v0

v1 whole, which is shorter than its diff:
```python
import functools
import math

import jax
import jax.numpy as jnp
import ml_dtypes
import numpy as np
from jax import lax
from jax.experimental import pallas as pl
from jax.experimental.pallas import tpu as pltpu
from jax.sharding import PartitionSpec as P

sample_scale = 2.0 ** (-29)
wrap_count = 32768
LANES = 128
KERNEL_BYTES = 55_800_000
PADDING = 1_200_000
MESH = pl.DeviceIdType.MESH


def halves(table):
    high = table.astype(np.float32).astype(ml_dtypes.bfloat16)
    low = (table - high.astype(np.float64)).astype(np.float32).astype(ml_dtypes.bfloat16)
    return high, low


@functools.lru_cache(maxsize=None)
def tables(sample_length, chip_count):
    inner = LANES
    outer = sample_length // inner
    a = np.arange(outer)
    c = np.arange(inner)
    ang_o = 2 * np.pi * (np.outer(a, a) % outer) / outer
    ang_t = 2 * np.pi * (np.outer(a, c) % sample_length) / sample_length
    ang_i = 2 * np.pi * (np.outer(c, c) % inner) / inner
    fc, fs = np.cos(ang_o), -np.sin(ang_o)
    first = np.block([[fc, -fs], [fs, fc]])
    second = np.block([[-fs, -fc], [fc, -fs]])
    wc, ws = np.cos(ang_i), -np.sin(ang_i)
    fh, fl = halves(np.block([[wc, ws], [-ws, wc]]))
    ih, il = halves(np.block([[wc, -ws], [ws, wc]]))
    bh, bl = halves(np.block([[fc, fs], [-fs, fc]]))
    ch, cl = halves(np.concatenate([fc, fs], axis=0))
    offsets = np.arange(sample_length).reshape(outer, inner)
    chips = offsets * chip_count // sample_length
    signs = 1 - 2 * ((offsets * 2 * chip_count // sample_length) % 2)
    starts = tuple(int(v) for v in chips[:, 0])
    within = chips - chips[:, :1]
    wide = np.concatenate([fh, fh, fl, ih, ih, il], axis=0)
    narrow = [first, second, np.cos(ang_t), -np.sin(ang_t), bh, bl,
              np.concatenate([ch, cl], axis=1), within, signs]
    narrow = np.concatenate([np.asarray(t, np.float32) for t in narrow], axis=0)
    return wide, narrow, starts


def padded(table, size):
    extra = -(-size // (table.shape[1] * table.dtype.itemsize)) - table.shape[0]
    return np.pad(table, ((0, max(extra, 0)), (0, 0)))


def split(value):
    high = value.astype(jnp.bfloat16)
    low = (value - high.astype(jnp.float32)).astype(jnp.bfloat16)
    return high, low


def mm(left, right):
    return jnp.dot(left, right, preferred_element_type=jnp.float32)


def flip(me, k, count):
    if count & (count - 1):
        return lax.rem(me + k, count)
    peer, bit = 0, 1
    while bit < count:
        peer = peer + ((me // bit + k // bit) % 2) * bit
        bit *= 2
    return peer


def back_flip(me, k, count):
    return lax.rem(me + count - k, count) if count & (count - 1) else flip(me, k, count)


def kernel(starts, outer, chip_count, cores, x_hbm, codes_hbm, dop_hbm, wide_hbm, narrow_hbm,
           power_ref, peak_ref, chips, dop_ref, wide, narrow, back,
           everyone, cpad, gath, cspec, rot, dtw, xs, spec, lagged, acc, peaks, mine,
           tab_sem, send_z, recv_z, send_tm, recv_tm, send_peak, recv_peak):
    inner = LANES
    tm_count, _, line, _, packed_rows, _ = everyone.shape
    dop_rows, sats = acc.shape[0], acc.shape[1]
    sample_length = outer * inner
    rows = outer // (cores * line)
    own = packed_rows // rows
    blocks = tm_count * own
    slots = spec.shape[0]
    me_tm, me_sat = lax.axis_index("tm"), lax.axis_index("sat")
    me_z, me_core = me_sat // cores, lax.rem(me_sat, cores)

    def place(z, core):
        return z * cores + core

    near = [(k, c) for k in range(line) for c in range(cores) if k or c]
    barrier = pltpu.get_barrier_semaphore()
    for k, c in near:
        target = place(flip(me_z, k, line), flip(me_core, c, cores))
        pl.semaphore_signal(barrier, inc=1, device_id={"sat": target}, device_id_type=MESH)
    for k in range(1, tm_count):
        for c in range(cores):
            target = place(me_z, flip(me_core, c, cores))
            pl.semaphore_signal(
                barrier, inc=1, device_id={"tm": flip(me_tm, k, tm_count), "sat": target}, device_id_type=MESH)

    pairs = ((x_hbm, everyone.at[me_tm, me_core, me_z]), (codes_hbm, chips), (dop_hbm, dop_ref),
             (narrow_hbm.at[pl.ds(0, narrow.shape[0])], narrow),
             (wide_hbm.at[pl.ds(0, wide.shape[0])], wide))
    loads = [pltpu.make_async_copy(h, t, tab_sem.at[i]) for i, (h, t) in enumerate(pairs)]
    for load in loads:
        load.start()

    def along_z(k, c):
        here = everyone.at[me_tm, me_core, me_z]
        target = place(flip(me_z, k, line), flip(me_core, c, cores))
        return pltpu.make_async_remote_copy(
            src_ref=here, dst_ref=here, send_sem=send_z.at[k * cores + c], recv_sem=recv_z.at[k * cores + c],
            device_id={"sat": target}, device_id_type=MESH)

    def from_z(k, c):
        there = everyone.at[me_tm, back_flip(me_core, c, cores), back_flip(me_z, k, line)]
        return pltpu.make_async_remote_copy(
            src_ref=there, dst_ref=there, send_sem=send_z.at[k * cores + c], recv_sem=recv_z.at[k * cores + c],
            device_id={"sat": me_sat}, device_id_type=MESH)

    def relay(k, z):
        for c in range(cores):
            piece = everyone.at[me_tm, me_core, z]
            pltpu.make_async_remote_copy(
                src_ref=piece, dst_ref=piece, send_sem=send_tm.at[k - 1], recv_sem=recv_tm.at[k - 1],
                device_id={"tm": flip(me_tm, k, tm_count), "sat": place(me_z, flip(me_core, c, cores))},
                device_id_type=MESH).start()

    def whole_group(k, at):
        return pltpu.make_async_remote_copy(
            src_ref=everyone.at[at], dst_ref=everyone.at[at], send_sem=send_tm.at[k - 1],
            recv_sem=recv_tm.at[k - 1], device_id={"tm": flip(me_tm, k, tm_count)}, device_id_type=MESH)

    def share_peak(k):
        return pltpu.make_async_remote_copy(
            src_ref=mine, dst_ref=peaks.at[k - 1], send_sem=send_peak.at[k - 1],
            recv_sem=recv_peak.at[k - 1], device_id={"tm": flip(me_tm, k, tm_count)}, device_id_type=MESH)

    early = range(1, max(tm_count - 1, 2)) if tm_count > 1 else ()
    late = [k for k in range(1, tm_count) if k not in early]

    loads[0].wait()
    pl.semaphore_wait(barrier, len(near) + (tm_count - 1) * cores)
    for k, c in reversed(near):
        along_z(k, c).start()
    for k in early:
        relay(k, me_z)

    loads[1].wait()
    cpad[...] = jnp.zeros_like(cpad)
    cpad[0:sats, 0:chip_count] = chips[...].astype(jnp.float32)
    for n1 in range(outer):
        base = starts[n1] // LANES * LANES
        shift = starts[n1] - base
        piece = cpad[:, base:base + 2 * LANES]
        if shift:
            piece = pltpu.roll(piece, 2 * LANES - shift, 1)
        for s in range(sats):
            gath[s, n1:n1 + 1, :] = piece[s:s + 1, :LANES]
    for load in loads[2:]:
        load.wait()

    cut = [0]

    def take(count):
        cut.append(cut[-1] + count)
        return narrow[cut[-2]:cut[-1]]

    first, second = take(2 * outer), take(2 * outer)
    t_re, t_im = take(outer), take(outer)
    bh, bl = take(2 * outer).astype(jnp.bfloat16), take(2 * outer).astype(jnp.bfloat16)
    back[...] = jnp.concatenate([bh, bh, bl], axis=1)
    code = take(2 * outer).astype(jnp.bfloat16)
    within = take(outer).astype(jnp.int32)
    signs = take(outer)
    t_at = 4 * outer
    fwd_ref = wide.at[pl.ds(0, 6 * inner)]
    inv_ref = wide.at[pl.ds(6 * inner, 6 * inner)]
    scale = math.sqrt(1.0 / (float(sample_length) ** 3 * blocks))
    for s in range(sats):
        rep = jnp.take_along_axis(gath[s], within, axis=1) * signs
        rep = rep.astype(jnp.bfloat16)
        y = mm(code, jnp.concatenate([rep, rep], axis=0))
        y_re, y_im = y[:outer], y[outer:]
        z = jnp.concatenate([y_re * t_re - y_im * t_im, y_re * t_im + y_im * t_re], axis=1)
        zh, zl = split(z)
        cspec[s] = mm(jnp.concatenate([zh, zl, zh], axis=1), fwd_ref[...]) * scale

    lane = lax.broadcasted_iota(jnp.int32, (8, inner), 1)
    row_of = lax.rem(lane, outer) * inner
    base_row = me_tm * dop_rows
    turn = 2.0 * math.pi / wrap_count
    bins = lax.broadcasted_iota(jnp.int32, (8, inner), 0)
    for f0 in range(0, dop_rows, 4):
        d = jnp.zeros((8, inner), jnp.int32)
        for f in range(f0, min(f0 + 4, dop_rows)):
            d = jnp.where(lax.rem(bins, 4) == f - f0, dop_ref[base_row + f], d)
        m = (jnp.where(bins < 4, row_of, lane) * d) & (wrap_count - 1)
        angle = m.astype(jnp.float32) * turn
        cosine, sine = jnp.cos(angle), -jnp.sin(angle)
        for f in range(f0, min(f0 + 4, dop_rows)):
            i = f - f0
            c1, s1 = cosine[i:i + 1] * sample_scale, sine[i:i + 1] * sample_scale
            c2, s2 = cosine[i + 4:i + 5], sine[i + 4:i + 5]
            mh, ml = split(first * c1 + second * s1)
            rot[f] = jnp.concatenate([mh, mh, ml], axis=1)
            dtw[f, 0] = t_re * c2 - t_im * s2
            dtw[f, 1] = t_re * s2 + t_im * c2
    acc[...] = jnp.zeros_like(acc)

    for k in range(1, line):
        from_z(k, 0).wait_recv()
        for j in early:
            relay(j, back_flip(me_z, k, line))
    for j in late:
        for k in range(line):
            relay(j, back_flip(me_z, k, line))
    for k, c in near:
        if c:
            from_z(k, c).wait_recv()

    def arrive(j):
        g = back_flip(me_tm, j, tm_count)
        for blk in range(own):
            parts = [everyone[g, q % cores, q // cores, part, pl.ds(blk, rows, stride=own), :]
                     for part in range(2) for q in range(cores * line)]
            x = jnp.concatenate(parts, axis=0).astype(jnp.float32)
            xh, xl = split(x)
            at = slice(blk * inner, (blk + 1) * inner)
            xs[0:2 * outer, at] = xh
            xs[2 * outer:4 * outer, at] = xl
            xs[4 * outer:6 * outer, at] = xh

    def rotate(f):
        return mm(rot[f], xs[...])

    def spectrum(f, y):
        u_re, u_im = dtw[f, 0], dtw[f, 1]
        zs = []
        for blk in range(own):
            y_re = y[:outer, blk * inner:(blk + 1) * inner]
            y_im = y[outer:, blk * inner:(blk + 1) * inner]
            zs.append(jnp.concatenate([y_re * u_re - y_im * u_im, y_re * u_im + y_im * u_re], axis=1))
        zh, zl = split(jnp.concatenate(zs, axis=0))
        spec[f % slots] = mm(jnp.concatenate([zh, zl, zh], axis=1), fwd_ref[...])

    def cross(f):
        crosses = []
        for s in range(sats):
            k_re, k_im = cspec[s, :, :inner], cspec[s, :, inner:]
            for blk in range(own):
                s_re = spec[f % slots, blk * outer:(blk + 1) * outer, :inner]
                s_im = spec[f % slots, blk * outer:(blk + 1) * outer, inner:]
                crosses.append(jnp.concatenate(
                    [s_re * k_re + s_im * k_im, s_im * k_re - s_re * k_im], axis=1))
        ch, cl = split(jnp.concatenate(crosses, axis=0))
        lag = mm(jnp.concatenate([ch, cl, ch], axis=1), inv_ref[...])
        w_re, w_im = narrow[t_at:t_at + outer], narrow[t_at + outer:t_at + 2 * outer]
        for s in range(sats):
            for blk in range(own):
                at = (s * own + blk) * outer
                l_re, l_im = lag[at:at + outer, :inner], lag[at:at + outer, inner:]
                wh, wl = split(jnp.concatenate(
                    [l_re * w_re + l_im * w_im, l_im * w_re - l_re * w_im], axis=0))
                to = slice(blk * inner, (blk + 1) * inner)
                lagged[f % slots, s, 0:2 * outer, to] = wh
                lagged[f % slots, s, 2 * outer:4 * outer, to] = wl

    def finish(f):
        for s in range(sats):
            high, low = lagged[f % slots, s, 0:2 * outer], lagged[f % slots, s, 2 * outer:4 * outer]
            out = mm(back[...], jnp.concatenate([high, low, high], axis=0))
            o_re, o_im = out[:outer], out[outer:]
            p = o_re * o_re + o_im * o_im
            total = p[:, :inner]
            for blk in range(1, own):
                total = total + p[:, blk * inner:(blk + 1) * inner]
            acc[f, s] += total

    def item(index):
        return index // dop_rows, index % dop_rows

    def step(at, c_index, b_index, a_index, total):
        if a_index is not None and 0 <= a_index < total:
            j, f = item(a_index)
            if f == 0:
                if a_index:
                    whole_group(at + j, back_flip(me_tm, at + j, tm_count)).wait_recv()
                arrive(at + j)
        if 0 <= c_index < total:
            finish(item(c_index)[1])
        if 0 <= a_index < total:
            y = rotate(item(a_index)[1])
        if 0 <= b_index < total:
            cross(item(b_index)[1])
        if 0 <= a_index < total:
            spectrum(item(a_index)[1], y)

    total = tm_count * dop_rows
    for t in range(-3, total):
        step(0, t, t + 2, t + 3, total)

    mine[...] = jnp.zeros_like(mine)
    for s in range(sats):
        top = acc[0, s]
        for f in range(1, dop_rows):
            top = jnp.maximum(top, acc[f, s])
        mine[s:s + 1, :] = jnp.max(top, axis=0, keepdims=True)
    for k in range(1, tm_count):
        share_peak(k).start()
    for f in range(dop_rows):
        for s in range(sats):
            power_ref[s, :, f, :] = acc[f, s]
    energy = jnp.zeros((8, inner), jnp.float32)
    for g in range(tm_count):
        x = everyone[g].astype(jnp.float32)
        energy = energy + jnp.sum((x * x).reshape(-1, 8, inner), axis=0)
    mean = jnp.sum(energy) * (sample_scale * sample_scale / float(blocks * sample_length))
    floor = jnp.maximum(mean, 0.25)
    for k, c in near:
        along_z(k, c).wait_send()
    for k in range(1, tm_count):
        whole_group(k, me_tm).wait_send()
    for k in range(1, tm_count):
        share_peak(k).wait()
    best = mine[...]
    for k in range(1, tm_count):
        best = jnp.maximum(best, peaks[k - 1])
    best = jnp.max(best, axis=1, keepdims=True)
    peak_ref[...] = jnp.broadcast_to(best / floor, peak_ref.shape)


def shards(samples, codes, dopplers):
    tm_count, sat_count = lax.axis_size("tm"), lax.axis_size("sat")
    own, segment = samples.shape[1], samples.shape[2]
    sample_length = segment * sat_count
    outer, rows = sample_length // LANES, segment // LANES
    sats, chip_count = codes.shape
    dop_rows = dopplers.shape[0] // tm_count
    cores = 2 if sat_count % 2 == 0 else 1
    line = sat_count // cores
    wide, narrow, starts = tables(sample_length, chip_count)
    pad = (max(starts) // LANES + 2) * LANES
    pad = max(pad, -(-chip_count // LANES) * LANES)
    peak_rows = -(-sats // 8) * 8
    slots = dop_rows if dop_rows % 2 else 2
    vm = pl.BlockSpec(memory_space=pltpu.VMEM)
    hbm = pl.BlockSpec(memory_space=pltpu.HBM)
    dma = pltpu.SemaphoreType.DMA
    packed = samples.reshape(2, own, rows, LANES).transpose(0, 2, 1, 3).reshape(2, rows * own, LANES)
    power, peak = pl.pallas_call(
        functools.partial(kernel, starts, outer, chip_count, cores),
        out_shape=(
            jax.ShapeDtypeStruct((sats, outer, dop_rows, LANES), jnp.float32),
            jax.ShapeDtypeStruct((peak_rows, LANES), jnp.float32),
        ),
        in_specs=[hbm, hbm, hbm, hbm, hbm],
        out_specs=(vm, vm),
        scratch_shapes=[
            pltpu.VMEM(codes.shape, jnp.int32),
            pltpu.SMEM(dopplers.shape, jnp.int32),
            pltpu.VMEM(wide.shape, jnp.bfloat16),
            pltpu.VMEM(narrow.shape, jnp.float32),
            pltpu.VMEM((2 * outer, 6 * outer), jnp.bfloat16),
            pltpu.VMEM((tm_count, cores, line, 2, rows * own, LANES), jnp.int32),
            pltpu.VMEM((8, pad), jnp.float32),
            pltpu.VMEM((sats, outer, LANES), jnp.float32),
            pltpu.VMEM((sats, outer, 2 * LANES), jnp.float32),
            pltpu.VMEM((dop_rows, 2 * outer, 6 * outer), jnp.bfloat16),
            pltpu.VMEM((dop_rows, 2, outer, LANES), jnp.float32),
            pltpu.VMEM((6 * outer, own * LANES), jnp.bfloat16),
            pltpu.VMEM((slots, own * outer, 2 * LANES), jnp.float32),
            pltpu.VMEM((slots, sats, 4 * outer, own * LANES), jnp.bfloat16),
            pltpu.VMEM((dop_rows, sats, outer, LANES), jnp.float32),
            pltpu.VMEM((tm_count - 1, peak_rows, LANES), jnp.float32),
            pltpu.VMEM((peak_rows, LANES), jnp.float32),
            dma((5,)),
            dma((sat_count,)),
            dma((sat_count,)),
            dma((tm_count - 1,)),
            dma((tm_count - 1,)),
            dma((tm_count - 1,)),
            dma((tm_count - 1,)),
        ],
        compiler_params=pltpu.CompilerParams(
            vmem_limit_bytes=KERNEL_BYTES, collective_id=0, has_side_effects=True),
        name="search",
    )(packed, codes, dopplers, jnp.asarray(padded(wide, PADDING)), jnp.asarray(padded(narrow, PADDING)))
    power = power.transpose(2, 0, 1, 3).reshape(dop_rows, sats, sample_length)
    return power, peak[:sats, 0]


def solution(mesh):
    placed = (P(None, "tm", "sat"), P("sat", None), P())
    return jax.shard_map(
        shards,
        mesh=mesh,
        in_specs=placed,
        out_specs=(P("tm", "sat", None), P("sat")),
        check_vma=False,
    )
```

time: 35.5 us -> 27.8 us (0.78)
  Pallas kernels: 31 us -> 23.3 us
    pallas_call x1, Pallas kernels: 31 us -> 23.3 us  [shards(): pl.pallas_call(functools.partial(kernel, starts, outer, chip_count, cores...]
where the time goes in v1:
time: 27.8 us; the launch traced here: 27.5 us
  Pallas kernels  23.3 us (84%)
  local copies, waits for them, and re-layouts  3.58 us (13%)
  between operations  0.65 us (2%)
    pallas_call x1, Pallas kernels, shards(): pl.pallas_call(functools.partial(kernel, starts, outer, chip_count, cores...  23.3 us
    unnamed x7, local copies, waits for them, and re-layouts  2.95 us
    slice x1, local copies, waits for them, and re-layouts, shards(): return (power, peak[:sats, 0])  0.63 us

profile of v1, /device:TPU:0, one launch (start us, length us, event | category | flops | bytes accessed | tf_op | source)
XLA Modules:
  0.0 27.5 jit_solution(4322311975364336276)
XLA Ops:
  0.6 0.0 copy-start
  0.6 0.8 %copy-done = s32[3,4092]{1,0:T(4,128)S(1)} copy-done((s32[3,4092]{1,0:T(4,128)S(1)}, s32[3,4092]{1,0:T(4,128)}, u32[]{:S(2)}) %copy-start) | copy-done | bytes 49128
  1.5 0.0 copy-start.1
  1.5 0.7 %copy-done.1 = s32[2,2,1024]{2,1,0:T(2,128)S(1)} copy-done((s32[2,2,1024]{2,1,0:T(2,128)S(1)}, s32[2,2,1024]{2,1,0:T(2,128)}, u32[]{:S(2)}) %copy-start.1) | copy-done | bytes 16408
  2.2 0.0 copy-start.2
  2.2 0.7 %copy-done.2 = s32[16]{0:T(128)S(1)} copy-done((s32[16]{0:T(128)S(1)}, s32[16]{0:T(128)}, u32[]{:S(2)}) %copy-start.2) | copy-done | bytes 88
  2.8 23.3 %search.1 = (f32[3,64,4,128]{3,2,1,0:T(4,128)S(1)}, f32[8,128]{1,0:T(8,128)S(1)}) custom-call(s32[2,16,128]{2,1,0:T(8,128)S(1)} %bitcast.9, s32[3,4092]{1,0:T(4,128)S(1)} %copy-done, s32[16]{0:T(128)S(1)} %copy-done.2, bf16[2344,256]{1,0:T(8,128)(2,1)} %constant.4.clone.wide_hbm, f32[2344,128]{1,0:T(8,128)} %constant.5.clone.narrow_hbm), custom_call_target="tpu_custom_call" | custom-call | tf_op jit(solution)/shard_map/search/pallas_call | solution.py:364
  26.2 0.6 %slice_reduce_fusion = f32[3]{0:T(128)} fusion(f32[8,128]{1,0:T(8,128)S(1)} %get-tuple-element.5), kind=kLoop, calls=%fused_computation | loop fusion | bytes 24 | tf_op jit(solution)/shard_map/slice | solution.py:403
  26.8 0.7 %copy.10 = f32[4,3,8192]{2,0,1:T(4,128)} copy(f32[4,3,8192]{2,0,1:T(4,128)S(1)} %bitcast.8) | data formatting | bytes 786432
Async XLA Ops:
  0.6 0.8 %copy-start = (s32[3,4092]{1,0:T(4,128)S(1)}, s32[3,4092]{1,0:T(4,128)}, u32[]{:S(2)}) copy-start(s32[3,4092]{1,0:T(4,128)} %codes_hbm.1) | copy-start | bytes 147316
  1.5 0.7 %copy-start.1 = (s32[2,2,1024]{2,1,0:T(2,128)S(1)}, s32[2,2,1024]{2,1,0:T(2,128)}, u32[]{:S(2)}) copy-start(s32[2,2,1024]{2,1,0:T(2,128)} %param.5) | copy-start | bytes 49156
  2.2 0.7 %copy-start.2 = (s32[16]{0:T(128)S(1)}, s32[16]{0:T(128)}, u32[]{:S(2)}) copy-start(s32[16]{0:T(128)} %dop_hbm.1) | copy-start | bytes 196

commit v2 on v1

--- a/solution.py
+++ b/solution.py
@@ -85,7 +85,8 @@
 def kernel(starts, outer, chip_count, cores, x_hbm, codes_hbm, dop_hbm, wide_hbm, narrow_hbm,
            power_ref, peak_ref, chips, dop_ref, wide, narrow, back,
            everyone, cpad, gath, cspec, rot, dtw, xs, spec, lagged, acc, peaks, mine,
-           tab_sem, send_z, recv_z, send_tm, recv_tm, send_peak, recv_peak):
+           tab_sem, send_z, recv_z, send_twin, recv_twin, send_far, recv_far, send_tm, recv_tm,
+           send_peak, recv_peak):
     inner = LANES
     tm_count, _, line, _, packed_rows, _ = everyone.shape
     dop_rows, sats = acc.shape[0], acc.shape[1]
@@ -100,9 +101,17 @@
     def place(z, core):
         return z * cores + core
 
-    near = [(k, c) for k in range(line) for c in range(cores) if k or c]
+    pairs = ((x_hbm, everyone.at[me_tm, me_core, me_z]), (codes_hbm, chips), (dop_hbm, dop_ref),
+             (narrow_hbm.at[pl.ds(0, narrow.shape[0])], narrow),
+             (wide_hbm.at[pl.ds(0, wide.shape[0])], wide))
+    loads = [pltpu.make_async_copy(h, t, tab_sem.at[i]) for i, (h, t) in enumerate(pairs)]
+    loads[0].start()
+
+    around = [(k, c) for k in range(line) for c in range(cores) if k or c]
+    far = [tm_count - 1] if tm_count > 2 else []
+    near = [k for k in range(1, tm_count) if k not in far]
     barrier = pltpu.get_barrier_semaphore()
-    for k, c in near:
+    for k, c in reversed(around):
         target = place(flip(me_z, k, line), flip(me_core, c, cores))
         pl.semaphore_signal(barrier, inc=1, device_id={"sat": target}, device_id_type=MESH)
     for k in range(1, tm_count):
@@ -111,31 +120,56 @@
             pl.semaphore_signal(
                 barrier, inc=1, device_id={"tm": flip(me_tm, k, tm_count), "sat": target}, device_id_type=MESH)
 
-    pairs = ((x_hbm, everyone.at[me_tm, me_core, me_z]), (codes_hbm, chips), (dop_hbm, dop_ref),
-             (narrow_hbm.at[pl.ds(0, narrow.shape[0])], narrow),
-             (wide_hbm.at[pl.ds(0, wide.shape[0])], wide))
-    loads = [pltpu.make_async_copy(h, t, tab_sem.at[i]) for i, (h, t) in enumerate(pairs)]
-    for load in loads:
+    for load in loads[1:]:
         load.start()
 
-    def along_z(k, c):
-        here = everyone.at[me_tm, me_core, me_z]
+    def pass_on(piece, sends, recvs, at, k, c):
         target = place(flip(me_z, k, line), flip(me_core, c, cores))
         return pltpu.make_async_remote_copy(
-            src_ref=here, dst_ref=here, send_sem=send_z.at[k * cores + c], recv_sem=recv_z.at[k * cores + c],
+            src_ref=piece, dst_ref=piece, send_sem=sends.at[at], recv_sem=recvs.at[at],
             device_id={"sat": target}, device_id_type=MESH)
 
-    def from_z(k, c):
-        there = everyone.at[me_tm, back_flip(me_core, c, cores), back_flip(me_z, k, line)]
+    def my_piece(z):
+        return everyone.at[me_tm, me_core, z]
+
+    def along_z(k):
+        return pass_on(my_piece(me_z), send_z, recv_z, k, k, 0)
+
+    def from_z(k):
+        return pass_on(my_piece(back_flip(me_z, k, line)), send_z, recv_z, k, k, 0)
+
+    def to_twin(k):
+        return pass_on(my_piece(back_flip(me_z, k, line)), send_twin, recv_twin, k, 0, 1)
+
+    def from_twin(k):
+        piece = everyone.at[me_tm, back_flip(me_core, 1, cores), back_flip(me_z, k, line)]
+        return pass_on(piece, send_twin, recv_twin, k, 0, 1)
+
+    def far_group(k):
+        return back_flip(me_tm, k, tm_count)
+
+    def to_far(k):
         return pltpu.make_async_remote_copy(
-            src_ref=there, dst_ref=there, send_sem=send_z.at[k * cores + c], recv_sem=recv_z.at[k * cores + c],
-            device_id={"sat": me_sat}, device_id_type=MESH)
+            src_ref=my_piece(me_z), dst_ref=my_piece(me_z), send_sem=send_far.at[0], recv_sem=recv_far.at[0],
+            device_id={"tm": flip(me_tm, k, tm_count)}, device_id_type=MESH)
+
+    def from_far(k):
+        piece = everyone.at[far_group(k), me_core, me_z]
+        return pltpu.make_async_remote_copy(
+            src_ref=piece, dst_ref=piece, send_sem=send_far.at[0], recv_sem=recv_far.at[0],
+            device_id={"tm": flip(me_tm, k, tm_count)}, device_id_type=MESH)
+
+    def spread_far(j, k, c):
+        return pass_on(everyone.at[far_group(j), me_core, me_z], send_far, recv_far, k * cores + c, k, c)
+
+    def gather_far(j, k, c):
+        piece = everyone.at[far_group(j), back_flip(me_core, c, cores), back_flip(me_z, k, line)]
+        return pass_on(piece, send_far, recv_far, k * cores + c, k, c)
 
     def relay(k, z):
         for c in range(cores):
-            piece = everyone.at[me_tm, me_core, z]
             pltpu.make_async_remote_copy(
-                src_ref=piece, dst_ref=piece, send_sem=send_tm.at[k - 1], recv_sem=recv_tm.at[k - 1],
+                src_ref=my_piece(z), dst_ref=my_piece(z), send_sem=send_tm.at[k - 1], recv_sem=recv_tm.at[k - 1],
                 device_id={"tm": flip(me_tm, k, tm_count), "sat": place(me_z, flip(me_core, c, cores))},
                 device_id_type=MESH).start()
 
@@ -149,15 +183,16 @@
             src_ref=mine, dst_ref=peaks.at[k - 1], send_sem=send_peak.at[k - 1],
             recv_sem=recv_peak.at[k - 1], device_id={"tm": flip(me_tm, k, tm_count)}, device_id_type=MESH)
 
-    early = range(1, max(tm_count - 1, 2)) if tm_count > 1 else ()
-    late = [k for k in range(1, tm_count) if k not in early]
-
     loads[0].wait()
-    pl.semaphore_wait(barrier, len(near) + (tm_count - 1) * cores)
-    for k, c in reversed(near):
-        along_z(k, c).start()
-    for k in early:
-        relay(k, me_z)
+    pl.semaphore_wait(barrier, len(around) + (tm_count - 1) * cores)
+    for k in reversed(range(1, line)):
+        along_z(k).start()
+    for j in far:
+        to_far(j).start()
+    for j in near:
+        relay(j, me_z)
+    if cores > 1:
+        to_twin(0).start()
 
     loads[1].wait()
     cpad[...] = jnp.zeros_like(cpad)
@@ -222,15 +257,19 @@
     acc[...] = jnp.zeros_like(acc)
 
     for k in range(1, line):
-        from_z(k, 0).wait_recv()
-        for j in early:
+        from_z(k).wait_recv()
+        if cores > 1:
+            to_twin(k).start()
+        for j in near:
             relay(j, back_flip(me_z, k, line))
-    for j in late:
+        if k == line // 2:
+            for j in far:
+                from_far(j).wait_recv()
+                for n, c in around:
+                    spread_far(j, n, c).start()
+    if cores > 1:
         for k in range(line):
-            relay(j, back_flip(me_z, k, line))
-    for k, c in near:
-        if c:
-            from_z(k, c).wait_recv()
+            from_twin(k).wait_recv()
 
     def arrive(j):
         g = back_flip(me_tm, j, tm_count)
@@ -290,28 +329,39 @@
                 total = total + p[:, blk * inner:(blk + 1) * inner]
             acc[f, s] += total
 
-    def item(index):
-        return index // dop_rows, index % dop_rows
-
-    def step(at, c_index, b_index, a_index, total):
-        if a_index is not None and 0 <= a_index < total:
-            j, f = item(a_index)
+    def step(f, forward, middle, last):
+        if last:
+            finish((f - 3) % dop_rows)
+        if forward:
+            y = rotate(f)
+        if middle:
+            cross((f - 1) % dop_rows)
+        if forward:
+            spectrum(f, y)
+
+    def group(j, first=False):
+        for f in range(dop_rows):
             if f == 0:
-                if a_index:
-                    whole_group(at + j, back_flip(me_tm, at + j, tm_count)).wait_recv()
-                arrive(at + j)
-        if 0 <= c_index < total:
-            finish(item(c_index)[1])
-        if 0 <= a_index < total:
-            y = rotate(item(a_index)[1])
-        if 0 <= b_index < total:
-            cross(item(b_index)[1])
-        if 0 <= a_index < total:
-            spectrum(item(a_index)[1], y)
-
-    total = tm_count * dop_rows
-    for t in range(-3, total):
-        step(0, t, t + 2, t + 3, total)
+                arrive(j)
+            step(f, True, not first or f >= 1, not first or f >= 3)
+
+    def near_group(j, carry):
+        whole_group(j, back_flip(me_tm, j, tm_count)).wait_recv()
+        group(j)
+        return carry
+
+    group(0, True)
+    if len(near) <= 3:
+        for j in near:
+            near_group(j, 0)
+    else:
+        lax.fori_loop(1, len(near) + 1, near_group, 0)
+    for j in far:
+        for n, c in around:
+            gather_far(j, n, c).wait_recv()
+        group(j)
+    for f in range(3):
+        step(f, False, f == 0, True)
 
     mine[...] = jnp.zeros_like(mine)
     for s in range(sats):
@@ -330,17 +380,41 @@
         energy = energy + jnp.sum((x * x).reshape(-1, 8, inner), axis=0)
     mean = jnp.sum(energy) * (sample_scale * sample_scale / float(blocks * sample_length))
     floor = jnp.maximum(mean, 0.25)
-    for k, c in near:
-        along_z(k, c).wait_send()
-    for k in range(1, tm_count):
+    for k in range(1, line):
+        along_z(k).wait_send()
+    if cores > 1:
+        for k in range(line):
+            to_twin(k).wait_send()
+    for j in far:
+        to_far(j).wait_send()
+        for n, c in around:
+            spread_far(j, n, c).wait_send()
+    for k in near:
         whole_group(k, me_tm).wait_send()
     for k in range(1, tm_count):
         share_peak(k).wait()
     best = mine[...]
     for k in range(1, tm_count):
         best = jnp.maximum(best, peaks[k - 1])
-    best = jnp.max(best, axis=1, keepdims=True)
-    peak_ref[...] = jnp.broadcast_to(best / floor, peak_ref.shape)
+    peak_ref[...] = best / floor
+
+
+def stay(value):
+    return pltpu.with_memory_space_constraint(value, pltpu.HBM)
+
+
+def emit(power_ref, peak_ref, power_hbm, detection_hbm, detection, sems):
+    copy = pltpu.make_async_copy(power_ref, power_hbm, sems.at[0])
+    copy.start()
+    best = jnp.max(peak_ref[...], axis=1, keepdims=True)
+    shape = peak_ref.shape
+    on = lax.broadcasted_iota(jnp.int32, shape, 0) == lax.broadcasted_iota(jnp.int32, shape, 1)
+    row = jnp.sum(jnp.where(on, best, 0.0), axis=0)
+    detection[...] = row[:detection.shape[0]]
+    small = pltpu.make_async_copy(detection, detection_hbm, sems.at[1])
+    small.start()
+    copy.wait()
+    small.wait()
 
 
 def shards(samples, codes, dopplers):
@@ -388,6 +462,10 @@
             pltpu.VMEM((tm_count - 1, peak_rows, LANES), jnp.float32),
             pltpu.VMEM((peak_rows, LANES), jnp.float32),
             dma((5,)),
+            dma((line,)),
+            dma((line,)),
+            dma((line,)),
+            dma((line,)),
             dma((sat_count,)),
             dma((sat_count,)),
             dma((tm_count - 1,)),
@@ -398,9 +476,21 @@
         compiler_params=pltpu.CompilerParams(
             vmem_limit_bytes=KERNEL_BYTES, collective_id=0, has_side_effects=True),
         name="search",
-    )(packed, codes, dopplers, jnp.asarray(padded(wide, PADDING)), jnp.asarray(padded(narrow, PADDING)))
+    )(stay(packed), stay(codes), stay(dopplers), jnp.asarray(padded(wide, PADDING)), jnp.asarray(padded(narrow, PADDING)))
+    power, detection = pl.pallas_call(
+        emit,
+        out_shape=(
+            jax.ShapeDtypeStruct(power.shape, jnp.float32),
+            jax.ShapeDtypeStruct((sats,), jnp.float32),
+        ),
+        in_specs=[vm, vm],
+        out_specs=(hbm, hbm),
+        scratch_shapes=[pltpu.VMEM((sats,), jnp.float32), dma((2,))],
+        compiler_params=pltpu.CompilerParams(vmem_limit_bytes=2_000_000),
+        name="emit",
+    )(power, peak)
     power = power.transpose(2, 0, 1, 3).reshape(dop_rows, sats, sample_length)
-    return power, peak[:sats, 0]
+    return power, detection
 
 
 def solution(mesh):

time: 27.8 us -> 23.3 us (0.84)
  local copies, waits for them, and re-layouts: 3.58 us -> 0 us
  Pallas kernels: 23.3 us -> 22.4 us
    unnamed x7 -> x0, local copies, waits for them, and re-layouts: 2.95 us -> none
    pallas_call x1, Pallas kernels: 23.3 us -> 21.6 us  [shards(): pl.pallas_call(functools.partial(kernel, starts, outer, chip_count, cores...]
    pallas_call x0 -> x1, Pallas kernels: none -> 0.77 us  [shards(): pl.pallas_call(emit, out_shape=(jax.ShapeDtypeStruct(power.shape, jnp.flo...]
    slice x1 -> x0, local copies, waits for them, and re-layouts: 0.63 us -> none  [shards(): return (power, peak[:sats, 0])]
where the time goes in v2:
time: 23.3 us; the launch traced here: 23 us
  Pallas kernels  22.4 us (96%)
  between operations  0.64 us (3%)
    pallas_call x1, Pallas kernels, shards(): pl.pallas_call(functools.partial(kernel, starts, outer, chip_count, cores...  21.6 us
    pallas_call x1, Pallas kernels, shards(): pl.pallas_call(emit, out_shape=(jax.ShapeDtypeStruct(power.shape, jnp.flo...  0.77 us

profile of v2, /device:TPU:0, one launch (start us, length us, event | category | flops | bytes accessed | tf_op | source)
XLA Modules:
  0.0 23.0 jit_solution(9649274559301712051)
XLA Ops:
  0.6 21.6 %search.1 = (f32[3,64,4,128]{3,2,1,0:T(4,128)S(1)}, f32[8,128]{1,0:T(8,128)S(1)}) custom-call(s32[2,16,128]{2,1,0:T(8,128)} %bitcast.8, s32[3,4092]{1,0:T(4,128)} %codes_hbm.1, s32[16]{0:T(128)} %dop_hbm.1, bf16[2344,256]{1,0:T(8,128)(2,1)} %constant.4.clone.wide_hbm, f32[2344,128]{1,0:T(8,128)} %constant.5.clone.narrow_hbm), custom_call_target="tpu_custom_call" | custom-call | tf_op jit(solution)/shard_map/search/pallas_call | solution.py:438
  22.2 0.8 %emit.1 = (f32[3,64,4,128]{3,2,1,0:T(4,128)}, f32[3]{0:T(128)}) custom-call(f32[3,64,4,128]{3,2,1,0:T(4,128)S(1)} %get-tuple-element.6.power_ref, f32[8,128]{1,0:T(8,128)S(1)} %get-tuple-element.7.peak_ref), custom_call_target="tpu_custom_call" | custom-call | tf_op jit(solution)/shard_map/emit/pallas_call | solution.py:480

commit v3 on v2

--- a/solution.py
+++ b/solution.py
@@ -25,7 +25,7 @@
 
 
 @functools.lru_cache(maxsize=None)
-def tables(sample_length, chip_count):
+def tables(sample_length, chip_count, rows):
     inner = LANES
     outer = sample_length // inner
     a = np.arange(outer)
@@ -39,16 +39,33 @@
     wc, ws = np.cos(ang_i), -np.sin(ang_i)
     fh, fl = halves(np.block([[wc, ws], [-ws, wc]]))
     ih, il = halves(np.block([[wc, -ws], [ws, wc]]))
-    bh, bl = halves(np.block([[fc, fs], [-fs, fc]]))
-    ch, cl = halves(np.concatenate([fc, fs], axis=0))
+    full = np.block([[fc, fs], [-fs, fc]])
+    half, span = outer // 2, rows // 2
+    low = np.concatenate([np.arange(0, half, 2), np.arange(1, half, 2)])
+    order = np.concatenate([low, low + half])
+    both = np.concatenate([low, low + outer])
+    spot = np.arange(outer)
+    base = spot // rows * rows + spot % span * 2
+    part = spot % rows // span
+    column = np.concatenate([base, base + 1])
+    picked = np.concatenate([part, part]) * outer + column
+    first, second = first[both][:, picked], second[both][:, picked]
+    keep = np.concatenate([np.arange(half), np.arange(half) + outer])
+    backs = []
+    for parity in range(2):
+        side = np.arange(parity, outer, 2)
+        bh, bl = halves(full[keep][:, np.concatenate([side, side + outer])])
+        backs.append(np.concatenate([bh, bl], axis=1))
+    ch, cl = halves(np.concatenate([fc[order], fs[order]], axis=0))
     offsets = np.arange(sample_length).reshape(outer, inner)
     chips = offsets * chip_count // sample_length
     signs = 1 - 2 * ((offsets * 2 * chip_count // sample_length) % 2)
     starts = tuple(int(v) for v in chips[:, 0])
     within = chips - chips[:, :1]
     wide = np.concatenate([fh, fh, fl, ih, ih, il], axis=0)
-    narrow = [first, second, np.cos(ang_t), -np.sin(ang_t), bh, bl,
-              np.concatenate([ch, cl], axis=1), within, signs]
+    ang_t = ang_t[order]
+    narrow = [first, second, np.cos(ang_t), -np.sin(ang_t), *backs,
+              np.concatenate([ch, cl], axis=1), within, signs, np.tile(column * inner, (8, 1))]
     narrow = np.concatenate([np.asarray(t, np.float32) for t in narrow], axis=0)
     return wide, narrow, starts
 
@@ -62,6 +79,19 @@
     high = value.astype(jnp.bfloat16)
     low = (value - high.astype(jnp.float32)).astype(jnp.bfloat16)
     return high, low
+
+
+def rest(value):
+    return value - value.astype(jnp.bfloat16).astype(jnp.float32)
+
+
+def three(pieces, table):
+    value = jnp.concatenate([jnp.concatenate(row, axis=1) for row in pieces], axis=0)
+    low = jnp.concatenate([jnp.concatenate([rest(p) for p in row], axis=1) for row in pieces], axis=0)
+    high, low = value.astype(jnp.bfloat16), low.astype(jnp.bfloat16)
+    depth = high.shape[1]
+    top, bottom = table[0:depth], table[2 * depth:3 * depth]
+    return mm(high, top) + mm(low, top) + mm(high, bottom)
 
 
 def mm(left, right):
@@ -88,11 +118,12 @@
            tab_sem, send_z, recv_z, send_twin, recv_twin, send_far, recv_far, send_tm, recv_tm,
            send_peak, recv_peak):
     inner = LANES
-    tm_count, _, line, _, packed_rows, _ = everyone.shape
+    tm_count, _, line, packed_rows, _ = everyone.shape
     dop_rows, sats = acc.shape[0], acc.shape[1]
     sample_length = outer * inner
     rows = outer // (cores * line)
-    own = packed_rows // rows
+    own = packed_rows // (2 * rows)
+    half = outer // 2
     blocks = tm_count * own
     slots = spec.shape[0]
     me_tm, me_sat = lax.axis_index("tm"), lax.axis_index("sat")
@@ -214,14 +245,17 @@
         cut.append(cut[-1] + count)
         return narrow[cut[-2]:cut[-1]]
 
-    first, second = take(2 * outer), take(2 * outer)
+    first, second = take(outer), take(outer)
     t_re, t_im = take(outer), take(outer)
-    bh, bl = take(2 * outer).astype(jnp.bfloat16), take(2 * outer).astype(jnp.bfloat16)
-    back[...] = jnp.concatenate([bh, bh, bl], axis=1)
+    for parity in range(2):
+        table = take(outer)
+        bh, bl = table[:, :outer], table[:, outer:]
+        back[parity] = jnp.concatenate([bh, bh, bl], axis=1).astype(jnp.bfloat16)
     code = take(2 * outer).astype(jnp.bfloat16)
     within = take(outer).astype(jnp.int32)
     signs = take(outer)
-    t_at = 4 * outer
+    row_of = take(8).astype(jnp.int32)
+    t_at = 2 * outer
     fwd_ref = wide.at[pl.ds(0, 6 * inner)]
     inv_ref = wide.at[pl.ds(6 * inner, 6 * inner)]
     scale = math.sqrt(1.0 / (float(sample_length) ** 3 * blocks))
@@ -235,7 +269,6 @@
         cspec[s] = mm(jnp.concatenate([zh, zl, zh], axis=1), fwd_ref[...]) * scale
 
     lane = lax.broadcasted_iota(jnp.int32, (8, inner), 1)
-    row_of = lax.rem(lane, outer) * inner
     base_row = me_tm * dop_rows
     turn = 2.0 * math.pi / wrap_count
     bins = lax.broadcasted_iota(jnp.int32, (8, inner), 0)
@@ -250,8 +283,11 @@
             i = f - f0
             c1, s1 = cosine[i:i + 1] * sample_scale, sine[i:i + 1] * sample_scale
             c2, s2 = cosine[i + 4:i + 5], sine[i + 4:i + 5]
-            mh, ml = split(first * c1 + second * s1)
-            rot[f] = jnp.concatenate([mh, mh, ml], axis=1)
+            mix = first * c1 + second * s1
+            low = mix - mix.astype(jnp.bfloat16).astype(jnp.float32)
+            for parity in range(2):
+                at = slice(parity * outer, (parity + 1) * outer)
+                rot[f, parity] = jnp.concatenate([mix[:, at], mix[:, at], low[:, at]], axis=1).astype(jnp.bfloat16)
             dtw[f, 0] = t_re * c2 - t_im * s2
             dtw[f, 1] = t_re * s2 + t_im * c2
     acc[...] = jnp.zeros_like(acc)
@@ -273,71 +309,81 @@
 
     def arrive(j):
         g = back_flip(me_tm, j, tm_count)
-        for blk in range(own):
-            parts = [everyone[g, q % cores, q // cores, part, pl.ds(blk, rows, stride=own), :]
-                     for part in range(2) for q in range(cores * line)]
-            x = jnp.concatenate(parts, axis=0).astype(jnp.float32)
-            xh, xl = split(x)
-            at = slice(blk * inner, (blk + 1) * inner)
-            xs[0:2 * outer, at] = xh
-            xs[2 * outer:4 * outer, at] = xl
-            xs[4 * outer:6 * outer, at] = xh
+        for parity in range(2):
+            cols = []
+            for blk in range(own):
+                parts = [everyone[g, q % cores, q // cores, pl.ds(parity * own + blk, rows, stride=2 * own), :]
+                         for q in range(cores * line)]
+                cols.append(jnp.concatenate(parts, axis=0))
+            xh, xl = split(jnp.concatenate(cols, axis=1).astype(jnp.float32))
+            xs[parity, 0:outer] = xh
+            xs[parity, outer:2 * outer] = xl
 
     def rotate(f):
-        return mm(rot[f], xs[...])
-
-    def spectrum(f, y):
+        sides = []
+        for parity in range(2):
+            high, low = xs[parity, 0:outer], xs[parity, outer:2 * outer]
+            sides.append(mm(rot[f, parity], jnp.concatenate([high, low, high], axis=0)))
+        return sides
+
+    def spectrum(f, sides):
         u_re, u_im = dtw[f, 0], dtw[f, 1]
+        plus, minus = sides[0] + sides[1], sides[0] - sides[1]
         zs = []
         for blk in range(own):
-            y_re = y[:outer, blk * inner:(blk + 1) * inner]
-            y_im = y[outer:, blk * inner:(blk + 1) * inner]
-            zs.append(jnp.concatenate([y_re * u_re - y_im * u_im, y_re * u_im + y_im * u_re], axis=1))
-        zh, zl = split(jnp.concatenate(zs, axis=0))
-        spec[f % slots] = mm(jnp.concatenate([zh, zl, zh], axis=1), fwd_ref[...])
-
-    def cross(f):
+            at = slice(blk * inner, (blk + 1) * inner)
+            y_re = jnp.concatenate([plus[:half, at], minus[:half, at]], axis=0)
+            y_im = jnp.concatenate([plus[half:, at], minus[half:, at]], axis=0)
+            zs.append((y_re * u_re - y_im * u_im, y_re * u_im + y_im * u_re))
+        spec[f % slots] = three(zs, fwd_ref)
+
+    def cross(f, s):
         crosses = []
-        for s in range(sats):
-            k_re, k_im = cspec[s, :, :inner], cspec[s, :, inner:]
-            for blk in range(own):
-                s_re = spec[f % slots, blk * outer:(blk + 1) * outer, :inner]
-                s_im = spec[f % slots, blk * outer:(blk + 1) * outer, inner:]
-                crosses.append(jnp.concatenate(
-                    [s_re * k_re + s_im * k_im, s_im * k_re - s_re * k_im], axis=1))
-        ch, cl = split(jnp.concatenate(crosses, axis=0))
-        lag = mm(jnp.concatenate([ch, cl, ch], axis=1), inv_ref[...])
+        k_re, k_im = cspec[s, :, :inner], cspec[s, :, inner:]
+        for blk in range(own):
+            s_re = spec[f % slots, blk * outer:(blk + 1) * outer, :inner]
+            s_im = spec[f % slots, blk * outer:(blk + 1) * outer, inner:]
+            crosses.append((s_re * k_re + s_im * k_im, s_im * k_re - s_re * k_im))
+        lag = three(crosses, inv_ref)
         w_re, w_im = narrow[t_at:t_at + outer], narrow[t_at + outer:t_at + 2 * outer]
-        for s in range(sats):
-            for blk in range(own):
-                at = (s * own + blk) * outer
-                l_re, l_im = lag[at:at + outer, :inner], lag[at:at + outer, inner:]
-                wh, wl = split(jnp.concatenate(
-                    [l_re * w_re + l_im * w_im, l_im * w_re - l_re * w_im], axis=0))
-                to = slice(blk * inner, (blk + 1) * inner)
-                lagged[f % slots, s, 0:2 * outer, to] = wh
-                lagged[f % slots, s, 2 * outer:4 * outer, to] = wl
-
-    def finish(f):
-        for s in range(sats):
-            high, low = lagged[f % slots, s, 0:2 * outer], lagged[f % slots, s, 2 * outer:4 * outer]
-            out = mm(back[...], jnp.concatenate([high, low, high], axis=0))
-            o_re, o_im = out[:outer], out[outer:]
+        quarter = outer // 4
+        cols = ([], [])
+        for blk in range(own):
+            at = blk * outer
+            l_re, l_im = lag[at:at + outer, :inner], lag[at:at + outer, inner:]
+            v_re, v_im = l_re * w_re + l_im * w_im, l_im * w_re - l_re * w_im
+            for parity in range(2):
+                one = slice(parity * quarter, (parity + 1) * quarter)
+                two = slice(half + parity * quarter, half + (parity + 1) * quarter)
+                cols[parity].append(jnp.concatenate([v_re[one], v_re[two], v_im[one], v_im[two]], axis=0))
+        for parity in range(2):
+            wh, wl = split(jnp.concatenate(cols[parity], axis=1))
+            lagged[f % slots, s, parity, 0:outer] = wh
+            lagged[f % slots, s, parity, outer:2 * outer] = wl
+
+    def finish(f, s):
+        sides = []
+        for parity in range(2):
+            high, low = lagged[f % slots, s, parity, 0:outer], lagged[f % slots, s, parity, outer:2 * outer]
+            sides.append(mm(back[parity], jnp.concatenate([high, low, high], axis=0)))
+        for at, out in ((0, sides[0] + sides[1]), (half, sides[0] - sides[1])):
+            o_re, o_im = out[:half], out[half:]
             p = o_re * o_re + o_im * o_im
             total = p[:, :inner]
             for blk in range(1, own):
                 total = total + p[:, blk * inner:(blk + 1) * inner]
-            acc[f, s] += total
+            acc[f, s, at:at + half] += total
 
     def step(f, forward, middle, last):
-        if last:
-            finish((f - 3) % dop_rows)
-        if forward:
-            y = rotate(f)
-        if middle:
-            cross((f - 1) % dop_rows)
-        if forward:
-            spectrum(f, y)
+        for s in range(sats):
+            if last:
+                finish((f - 3) % dop_rows, s)
+            if s == 0 and forward:
+                y = rotate(f)
+            if middle:
+                cross((f - 1) % dop_rows, s)
+            if s == max(sats - 2, 0) and forward:
+                spectrum(f, y)
 
     def group(j, first=False):
         for f in range(dop_rows):
@@ -345,20 +391,31 @@
                 arrive(j)
             step(f, True, not first or f >= 1, not first or f >= 3)
 
+    def await_near(j):
+        whole_group(j, back_flip(me_tm, j, tm_count)).wait_recv()
+
+    def await_far(j):
+        for n, c in around:
+            gather_far(j, n, c).wait_recv()
+
     def near_group(j, carry):
-        whole_group(j, back_flip(me_tm, j, tm_count)).wait_recv()
+        await_near(j)
         group(j)
         return carry
 
     group(0, True)
     if len(near) <= 3:
         for j in near:
-            near_group(j, 0)
+            await_near(j)
+            if j == len(near):
+                for k in far:
+                    await_far(k)
+            group(j)
     else:
         lax.fori_loop(1, len(near) + 1, near_group, 0)
+        for j in far:
+            await_far(j)
     for j in far:
-        for n, c in around:
-            gather_far(j, n, c).wait_recv()
         group(j)
     for f in range(3):
         step(f, False, f == 0, True)
@@ -426,7 +483,7 @@
     dop_rows = dopplers.shape[0] // tm_count
     cores = 2 if sat_count % 2 == 0 else 1
     line = sat_count // cores
-    wide, narrow, starts = tables(sample_length, chip_count)
+    wide, narrow, starts = tables(sample_length, chip_count, rows)
     pad = (max(starts) // LANES + 2) * LANES
     pad = max(pad, -(-chip_count // LANES) * LANES)
     peak_rows = -(-sats // 8) * 8
@@ -434,7 +491,7 @@
     vm = pl.BlockSpec(memory_space=pltpu.VMEM)
     hbm = pl.BlockSpec(memory_space=pltpu.HBM)
     dma = pltpu.SemaphoreType.DMA
-    packed = samples.reshape(2, own, rows, LANES).transpose(0, 2, 1, 3).reshape(2, rows * own, LANES)
+    packed = samples.reshape(2, own, rows, LANES).transpose(0, 2, 1, 3).reshape(2 * rows * own, LANES)
     power, peak = pl.pallas_call(
         functools.partial(kernel, starts, outer, chip_count, cores),
         out_shape=(
@@ -448,16 +505,16 @@
             pltpu.SMEM(dopplers.shape, jnp.int32),
             pltpu.VMEM(wide.shape, jnp.bfloat16),
             pltpu.VMEM(narrow.shape, jnp.float32),
-            pltpu.VMEM((2 * outer, 6 * outer), jnp.bfloat16),
-            pltpu.VMEM((tm_count, cores, line, 2, rows * own, LANES), jnp.int32),
+            pltpu.VMEM((2, outer, 3 * outer), jnp.bfloat16),
+            pltpu.VMEM((tm_count, cores, line, 2 * rows * own, LANES), jnp.int32),
             pltpu.VMEM((8, pad), jnp.float32),
             pltpu.VMEM((sats, outer, LANES), jnp.float32),
             pltpu.VMEM((sats, outer, 2 * LANES), jnp.float32),
-            pltpu.VMEM((dop_rows, 2 * outer, 6 * outer), jnp.bfloat16),
+            pltpu.VMEM((dop_rows, 2, outer, 3 * outer), jnp.bfloat16),
             pltpu.VMEM((dop_rows, 2, outer, LANES), jnp.float32),
-            pltpu.VMEM((6 * outer, own * LANES), jnp.bfloat16),
+            pltpu.VMEM((2, 2 * outer, own * LANES), jnp.bfloat16),
             pltpu.VMEM((slots, own * outer, 2 * LANES), jnp.float32),
-            pltpu.VMEM((slots, sats, 4 * outer, own * LANES), jnp.bfloat16),
+            pltpu.VMEM((slots, sats, 2, 2 * outer, own * LANES), jnp.bfloat16),
             pltpu.VMEM((dop_rows, sats, outer, LANES), jnp.float32),
             pltpu.VMEM((tm_count - 1, peak_rows, LANES), jnp.float32),
             pltpu.VMEM((peak_rows, LANES), jnp.float32),

time: 23.3 us -> 22.6 us (0.970)
  Pallas kernels: 22.4 us -> 21.7 us
    pallas_call x1, Pallas kernels: 21.6 us -> 20.9 us  [shards(): pl.pallas_call(functools.partial(kernel, starts, outer, chip_count, cores...]
where the time goes in v3:
time: 22.6 us; the launch traced here: 22.4 us
  Pallas kernels  21.7 us (96%)
  between operations  0.64 us (3%)
    pallas_call x1, Pallas kernels, shards(): pl.pallas_call(functools.partial(kernel, starts, outer, chip_count, cores...  20.9 us
    pallas_call x1, Pallas kernels, shards(): pl.pallas_call(emit, out_shape=(jax.ShapeDtypeStruct(power.shape, jnp.flo...  0.77 us

profile of v3, /device:TPU:0, one launch (start us, length us, event | category | flops | bytes accessed | tf_op | source)
XLA Modules:
  0.0 22.4 jit_solution(10314116466555053616)
XLA Ops:
  0.6 20.9 %search.1 = (f32[3,64,4,128]{3,2,1,0:T(4,128)S(1)}, f32[8,128]{1,0:T(8,128)S(1)}) custom-call(s32[32,128]{1,0:T(8,128)} %bitcast.8, s32[3,4092]{1,0:T(4,128)} %codes_hbm.1, s32[16]{0:T(128)} %dop_hbm.1, bf16[2344,256]{1,0:T(8,128)(2,1)} %constant.4.clone.wide_hbm, f32[2344,128]{1,0:T(8,128)} %constant.5.clone.narrow_hbm), custom_call_target="tpu_custom_call" | custom-call | tf_op jit(solution)/shard_map/search/pallas_call | solution.py:495
  21.6 0.8 %emit.1 = (f32[3,64,4,128]{3,2,1,0:T(4,128)}, f32[3]{0:T(128)}) custom-call(f32[3,64,4,128]{3,2,1,0:T(4,128)S(1)} %get-tuple-element.6.power_ref, f32[8,128]{1,0:T(8,128)S(1)} %get-tuple-element.7.peak_ref), custom_call_target="tpu_custom_call" | custom-call | tf_op jit(solution)/shard_map/emit/pallas_call | solution.py:537

commit v4 on v3

--- a/solution.py
+++ b/solution.py
@@ -91,7 +91,9 @@
     high, low = value.astype(jnp.bfloat16), low.astype(jnp.bfloat16)
     depth = high.shape[1]
     top, bottom = table[0:depth], table[2 * depth:3 * depth]
-    return mm(high, top) + mm(low, top) + mm(high, bottom)
+    count = high.shape[0]
+    pair = mm(jnp.concatenate([high, low], axis=0), top)
+    return pair[:count] + (pair[count:] + mm(high, bottom))
 
 
 def mm(left, right):
@@ -375,28 +377,24 @@
             acc[f, s, at:at + half] += total
 
     def step(f, forward, middle, last):
+        if forward:
+            y = rotate(f)
         for s in range(sats):
-            if last:
-                finish((f - 3) % dop_rows, s)
-            if s == 0 and forward:
-                y = rotate(f)
             if middle:
                 cross((f - 1) % dop_rows, s)
             if s == max(sats - 2, 0) and forward:
                 spectrum(f, y)
+            if last:
+                finish((f - 2) % dop_rows, s)
 
     def group(j, first=False):
         for f in range(dop_rows):
             if f == 0:
                 arrive(j)
-            step(f, True, not first or f >= 1, not first or f >= 3)
+            step(f, True, not first or f >= 1, not first or f >= 2)
 
     def await_near(j):
         whole_group(j, back_flip(me_tm, j, tm_count)).wait_recv()
-
-    def await_far(j):
-        for n, c in around:
-            gather_far(j, n, c).wait_recv()
 
     def near_group(j, carry):
         await_near(j)
@@ -407,17 +405,15 @@
     if len(near) <= 3:
         for j in near:
             await_near(j)
-            if j == len(near):
-                for k in far:
-                    await_far(k)
+        for j in near:
             group(j)
     else:
         lax.fori_loop(1, len(near) + 1, near_group, 0)
-        for j in far:
-            await_far(j)
     for j in far:
+        for n, c in around:
+            gather_far(j, n, c).wait_recv()
         group(j)
-    for f in range(3):
+    for f in range(2):
         step(f, False, f == 0, True)
 
     mine[...] = jnp.zeros_like(mine)
@@ -487,7 +483,7 @@
     pad = (max(starts) // LANES + 2) * LANES
     pad = max(pad, -(-chip_count // LANES) * LANES)
     peak_rows = -(-sats // 8) * 8
-    slots = dop_rows if dop_rows % 2 else 2
+    slots = max(dop_rows, 2)
     vm = pl.BlockSpec(memory_space=pltpu.VMEM)
     hbm = pl.BlockSpec(memory_space=pltpu.HBM)
     dma = pltpu.SemaphoreType.DMA

time: 22.6 us -> 22.4 us (level)
  no operation moved by 1% of the time
where the time goes in v4:
time: 22.4 us; the launch traced here: 22.2 us
  Pallas kernels  21.5 us (96%)
  between operations  0.64 us (3%)
    pallas_call x1, Pallas kernels, shards(): pl.pallas_call(functools.partial(kernel, starts, outer, chip_count, cores...  20.8 us
    pallas_call x1, Pallas kernels, shards(): pl.pallas_call(emit, out_shape=(jax.ShapeDtypeStruct(power.shape, jnp.flo...  0.77 us

profile of v4, /device:TPU:0, one launch (start us, length us, event | category | flops | bytes accessed | tf_op | source)
XLA Modules:
  0.0 22.2 jit_solution(17622084375400841656)
XLA Ops:
  0.6 20.8 %search.1 = (f32[3,64,4,128]{3,2,1,0:T(4,128)S(1)}, f32[8,128]{1,0:T(8,128)S(1)}) custom-call(s32[32,128]{1,0:T(8,128)} %bitcast.8, s32[3,4092]{1,0:T(4,128)} %codes_hbm.1, s32[16]{0:T(128)} %dop_hbm.1, bf16[2344,256]{1,0:T(8,128)(2,1)} %constant.4.clone.wide_hbm, f32[2344,128]{1,0:T(8,128)} %constant.5.clone.narrow_hbm), custom_call_target="tpu_custom_call" | custom-call | tf_op jit(solution)/shard_map/search/pallas_call | solution.py:491
  21.4 0.8 %emit.1 = (f32[3,64,4,128]{3,2,1,0:T(4,128)}, f32[3]{0:T(128)}) custom-call(f32[3,64,4,128]{3,2,1,0:T(4,128)S(1)} %get-tuple-element.6.power_ref, f32[8,128]{1,0:T(8,128)S(1)} %get-tuple-element.7.peak_ref), custom_call_target="tpu_custom_call" | custom-call | tf_op jit(solution)/shard_map/emit/pallas_call | solution.py:533

commit v5 on v4

--- a/solution.py
+++ b/solution.py
@@ -294,17 +294,21 @@
             dtw[f, 1] = t_re * s2 + t_im * c2
     acc[...] = jnp.zeros_like(acc)
 
-    for k in range(1, line):
+    inside = ((me_z + 1) // 2) % 2 if line == 4 else 0
+    for n in range(1, line):
+        k = n
+        if line == 4 and n > 1:
+            k = 2 + inside if n == 2 else 3 - inside
         from_z(k).wait_recv()
         if cores > 1:
             to_twin(k).start()
         for j in near:
             relay(j, back_flip(me_z, k, line))
-        if k == line // 2:
+        if n == line // 2:
             for j in far:
                 from_far(j).wait_recv()
-                for n, c in around:
-                    spread_far(j, n, c).start()
+                for i, c in around:
+                    spread_far(j, i, c).start()
     if cores > 1:
         for k in range(line):
             from_twin(k).wait_recv()

time: 22.4 us -> 22.4 us (level)
  no operation moved by 1% of the time
where the time goes in v5:
time: 22.4 us; the launch traced here: 22.2 us
  Pallas kernels  21.5 us (96%)
  between operations  0.64 us (3%)
    pallas_call x1, Pallas kernels, shards(): pl.pallas_call(functools.partial(kernel, starts, outer, chip_count, cores...  20.8 us
    pallas_call x1, Pallas kernels, shards(): pl.pallas_call(emit, out_shape=(jax.ShapeDtypeStruct(power.shape, jnp.flo...  0.77 us

profile of v5, /device:TPU:0, one launch (start us, length us, event | category | flops | bytes accessed | tf_op | source)
XLA Modules:
  0.0 22.2 jit_solution(16698701300211497961)
XLA Ops:
  0.6 20.8 %search.1 = (f32[3,64,4,128]{3,2,1,0:T(4,128)S(1)}, f32[8,128]{1,0:T(8,128)S(1)}) custom-call(s32[32,128]{1,0:T(8,128)} %bitcast.8, s32[3,4092]{1,0:T(4,128)} %codes_hbm.1, s32[16]{0:T(128)} %dop_hbm.1, bf16[2344,256]{1,0:T(8,128)(2,1)} %constant.4.clone.wide_hbm, f32[2344,128]{1,0:T(8,128)} %constant.5.clone.narrow_hbm), custom_call_target="tpu_custom_call" | custom-call | tf_op jit(solution)/shard_map/search/pallas_call | solution.py:495
  21.4 0.8 %emit.1 = (f32[3,64,4,128]{3,2,1,0:T(4,128)}, f32[3]{0:T(128)}) custom-call(f32[3,64,4,128]{3,2,1,0:T(4,128)S(1)} %get-tuple-element.6.power_ref, f32[8,128]{1,0:T(8,128)S(1)} %get-tuple-element.7.peak_ref), custom_call_target="tpu_custom_call" | custom-call | tf_op jit(solution)/shard_map/emit/pallas_call | solution.py:537
